TPU v7x, 32 devices: a whole 2x2x4 slice. The times are simulated.
32 devices in a mesh: blk: 8 (over y, x, core), ulysses: 4 (over z).
Axes of the slice: x: 2, y: 2, z: 4, core: 2. Of those that a mesh axis runs over, the one named last changes fastest.
Arguments:
- tokens: bfloat16 [2048, 3072], P(('blk', 'ulysses')), may hold values from -6 to 6
- mod_shift: float32 [3072], replicated, may hold values from -3 to 3
- mod_scale: float32 [3072], replicated, may hold values from -3 to 3
- mod_gate: float32 [3072], replicated, may hold values from 0.5 to 1.5
- qkv_weight: bfloat16 [3, 3072, 3072], P(None, None, 'ulysses'), may hold values from -0.109375 to 0.109375
- query_gain: float32 [128], replicated, may hold values from 1 to 16
- key_gain: float32 [128], replicated, may hold values from 1 to 16
- out_weight: bfloat16 [3072, 3072], P(None, 'ulysses'), may hold values from -0.109375 to 0.109375
Outputs:
- mixed: bfloat16 [2048, 3072], P(('blk', 'ulysses'))
All inputs are finite; a program needn't handle non-finite values.
Results may differ from a plain program's by a relative error of at most 0.013.
The roundings to bfloat16 on the way count: a program that leaves them out, or rounds other values in their place, can miss the bound.
Values may be sent and summed in bfloat16 or wider, within the bound.
No kernel may reach another device: no remote copies, remote signals or barrier semaphores. Data moves between devices by JAX's collectives and lax.ppermute only.
A program may use at most 128 MiB of HBM per device.

v0:
```python
import math
import jax
import jax.numpy as jnp
from jax import lax
from jax.sharding import PartitionSpec as P


def head_norm(projected, gain, factor):
    split = projected.reshape(projected.shape[0], -1, gain.shape[0])
    meansq = jnp.mean(split * split, axis=-1, keepdims=True)
    return (split * lax.rsqrt(meansq + 1e-06) * gain * factor).reshape(projected.shape)


def local(tokens, mod_shift, mod_scale, mod_gate, qkv_weight, query_gain, key_gain, out_weight):
    wide = tokens.astype(jnp.float32)
    center = jnp.mean(wide, axis=-1, keepdims=True)
    spread = jnp.mean((wide - center) ** 2, axis=-1, keepdims=True)
    normed = (wide - center) / jnp.sqrt(spread + 1e-06)
    modulated = (normed * (1.0 + mod_scale) + mod_shift).astype(jnp.bfloat16)
    head_size = query_gain.shape[0]
    local_width = qkv_weight.shape[2]
    heads_here = local_width // head_size
    factor = 1.0 / math.sqrt(head_size)
    sums = jnp.einsum(
        "rd,jde->jre",
        lax.all_gather(modulated, "ulysses", axis=0, tiled=True),
        qkv_weight,
        preferred_element_type=jnp.float32,
    )
    queries = head_norm(sums[0], query_gain, factor)
    keys = head_norm(sums[1], key_gain, 1.0)
    stacked = jnp.stack([queries, keys, sums[2]]).astype(jnp.bfloat16)
    queries, keys, values = (stacked[0], stacked[1], stacked[2])
    query_rows = queries.shape[0]
    query_heads = queries.reshape(query_rows, heads_here, head_size)
    start_state = (
        jnp.full((heads_here, query_rows), -1e30, jnp.float32),
        jnp.zeros((heads_here, query_rows), jnp.float32),
        jnp.zeros((heads_here, query_rows, head_size), jnp.float32),
    )
    key_part = lax.all_gather(keys, "blk", axis=0, tiled=True)
    value_part = lax.all_gather(values, "blk", axis=0, tiled=True)
    count = key_part.shape[0] // query_rows

    def step(position, state):
        highest, total, numerator = state
        key_block = lax.dynamic_slice_in_dim(key_part, position * query_rows, query_rows, 0)
        value_block = lax.dynamic_slice_in_dim(value_part, position * query_rows, query_rows, 0)
        key_block = key_block.reshape(query_rows, heads_here, head_size)
        value_block = value_block.reshape(query_rows, heads_here, head_size)
        scores = jnp.einsum(
            "qhd,khd->hqk", query_heads, key_block, preferred_element_type=jnp.float32
        )
        new_high = jnp.maximum(highest, jnp.max(scores, axis=-1))
        rescale = jnp.exp(highest - new_high)
        powers = jnp.exp(scores - new_high[..., None])
        total = total * rescale + jnp.sum(powers, axis=-1)
        numerator = numerator * rescale[..., None] + jnp.einsum(
            "hqk,khd->hqd",
            powers.astype(jnp.bfloat16),
            value_block,
            preferred_element_type=jnp.float32,
        )
        return (new_high, total, numerator)

    highest, total, numerator = lax.fori_loop(0, count, step, start_state)
    attended = (numerator / total[..., None]).transpose(1, 0, 2).reshape(query_rows, local_width)
    attended = attended.astype(jnp.bfloat16)
    columns = jnp.dot(
        lax.all_gather(attended, "ulysses", axis=1, tiled=True),
        out_weight,
        preferred_element_type=jnp.float32,
    )
    branch = lax.all_to_all(
        columns.astype(jnp.bfloat16), "ulysses", split_axis=0, concat_axis=1, tiled=True
    ).astype(columns.dtype)
    return (wide + mod_gate * branch).astype(jnp.bfloat16)


def solution(mesh):
    in_specs = (
        P(("blk", "ulysses"), None),
        P(),
        P(),
        P(),
        P(None, None, "ulysses"),
        P(),
        P(),
        P(None, "ulysses"),
    )
    out_specs = P(("blk", "ulysses"), None)
    return jax.shard_map(local, mesh=mesh, in_specs=in_specs, out_specs=out_specs, check_vma=False)
```

profile of v0, /device:TPU:0, one launch (start us, length us, event | category | flops | bytes accessed | tf_op | source)
XLA Modules:
  0.0 214.0 jit_solution(12685129563109106059)
XLA Ops:
  6.5 1.1 convert_reduce_fusion
  7.7 1.3 fusion.9
  9.0 0.7 broadcast_add_fusion
  9.7 2.0 fusion.12
  11.8 39.8 %all-gather.7.cloned.1.call-done = bf16[256,3072]{1,0:T(8,128)(2,1)} async-done(((bf16[64,3072]{1,0:T(8,128)(2,1)}), bf16[256,3072]{1,0:T(8,128)(2,1)}) %all-gather.7.cloned.1.call-update) | async-done | bytes 1572880 | tf_op jit(solution)/shard_map/all_gather | solution.py:26
  51.6 7.9 %convolution_bitcast_fusion = f32[3,256,768]{2,1,0:T(8,128)S(1)} fusion(bf16[3,3072,768]{2,1,0:T(8,128)(2,1)} %param.14, bf16[256,3072]{1,0:T(8,128)(2,1)} %all-gather.7.cloned.1.call-done), kind=kOutput, calls=%fused_computation.14 | convolution fusion | flops 3623878656 | bytes 18087936 | tf_op jit(solution)/shard_map/rd,jde->jre/dot_general | solution.py:24
  59.5 0.8 slice.32
  60.3 1.2 slice_multiply_fusion
  61.6 1.4 copy.30
  63.1 1.2 copy.31
  64.3 1.4 copy.28
  65.9 1.1 copy.29
  67.0 2.4 %multiply_convert_fusion = (bf16[1,256,768]{2,1,0:T(8,128)(2,1)S(1)}, bf16[1,256,768]{2,1,0:T(8,128)(2,1)}) fusion(f32[1,256,768]{2,1,0:T(8,128)} %copy.31, f32[3,256,768]{2,1,0:T(8,128)S(1)} %convolution_bitcast_fusion, f32[768]{0:T(1024)S(1)} %get-tuple-element.201, f32[768]{0:T(1024)S(1)} %get-tuple-element.202, f32[1,256,768]{2,1,0:T(8,128)} %copy.29), kind=kLoop, calls=%fused_computation.30 | loop fusion | flops 1376256 | bytes 3938304 | tf_op jit(solution)/shard_map/slice | solution.py:33
  69.9 21.6 %all-gather.13.cloned.1.call-done = bf16[1,2048,768]{2,1,0:T(8,128)(2,1)} async-done(((bf16[1,256,768]{2,1,0:T(8,128)(2,1)}), bf16[1,2048,768]{2,1,0:T(8,128)(2,1)}) %all-gather.13.cloned.1.call-update) | async-done | bytes 3145744 | tf_op jit(solution)/shard_map/all_gather | solution.py:42
  91.5 34.1 %all-gather.11.cloned.1.call-done = bf16[1,2048,768]{2,1,0:T(8,128)(2,1)} async-done(((bf16[1,256,768]{2,1,0:T(8,128)(2,1)}), bf16[1,2048,768]{2,1,0:T(8,128)(2,1)}) %all-gather.11.cloned.1.call-update) | async-done | bytes 3145744 | tf_op jit(solution)/shard_map/all_gather | solution.py:41
  125.6 23.6 %while.18 = (s32[]{:T(128)}, f32[6,256]{1,0:T(8,128)S(1)}, f32[6,256]{1,0:T(8,128)S(1)}, f32[6,256,128]{2,1,0:T(8,128)S(1)}, bf16[2048,768]{1,0:T(8,128)(2,1)}, ...) while((s32[]{:T(128)}, f32[6,256]{1,0:T(8,128)S(1)}, ...), condition=%wide.region_7.0_spmd.clone, body=%wide.region_4.0_spmd.clone.sunk | while | flops 203890176 | bytes 10715315 | solution.py:66
  125.6 1.2 constant_dynamic-slice_fusion.3
  127.1 0.4 bitcast_reduce_fusion.2
  127.8 0.7 convolution_add_fusion.2
  128.5 1.2 constant_dynamic-slice_fusion.3
  130.0 0.4 bitcast_reduce_fusion.2
  130.5 0.2 fusion.30
  130.7 0.7 convolution_add_fusion.2
  131.5 1.2 constant_dynamic-slice_fusion.3
  133.0 0.4 bitcast_reduce_fusion.2
  133.7 0.7 convolution_add_fusion.2
  134.4 1.2 constant_dynamic-slice_fusion.3
  135.9 0.4 bitcast_reduce_fusion.2
  136.6 0.7 convolution_add_fusion.2
  137.4 1.2 constant_dynamic-slice_fusion.3
  138.9 0.4 bitcast_reduce_fusion.2
  139.6 0.7 convolution_add_fusion.2
  140.3 1.2 constant_dynamic-slice_fusion.3
  141.8 0.4 bitcast_reduce_fusion.2
  142.5 0.7 convolution_add_fusion.2
  143.3 1.2 constant_dynamic-slice_fusion.3
  144.8 0.4 bitcast_reduce_fusion.2
  145.5 0.7 convolution_add_fusion.2
  146.2 1.2 constant_dynamic-slice_fusion.3
  147.7 0.4 bitcast_reduce_fusion.2
  148.4 0.7 convolution_add_fusion.2
  149.1 0.3 copy.36
  149.4 0.8 divide_convert_fusion
  150.2 37.2 %all-gather.9.cloned.1.call-done = bf16[256,3072]{0,1:T(8,128)(2,1)} async-done(((bf16[256,768]{0,1:T(8,128)(2,1)}), bf16[256,3072]{0,1:T(8,128)(2,1)}) %all-gather.9.cloned.1.call-update) | async-done | bytes 1572880 | tf_op jit(solution)/shard_map/all_gather | solution.py:70
  187.4 4.2 %convolution_convert_fusion = bf16[256,768]{1,0:T(8,128)(2,1)S(1)} fusion(bf16[256,3072]{0,1:T(8,128)(2,1)} %all-gather.9.cloned.1.call-done, bf16[3072,768]{1,0:T(8,128)(2,1)} %param.17), kind=kOutput, calls=%fused_computation.16 | convolution fusion | flops 1208156160 | bytes 6684672 | tf_op jit(solution)/shard_map/dot_general | solution.py:69
  191.7 13.9 %all_to_all.13 = bf16[4,64,768]{2,1,0:T(8,128)(2,1)S(1)} all-to-all(bf16[4,64,768]{2,1,0:T(8,128)(2,1)S(1)} %bitcast.69), channel_id=1, replica_groups=mesh['blk'=8,'ulysses'=4] {'ulysses'}, dimensions={0} | all-to-all | bytes 786432 | tf_op jit(solution)/shard_map/all_to_all | solution.py:74
  205.7 0.9 copy-done
  206.6 0.8 fusion.13
  (78 shorter events, 5.4 us)
Async XLA Ops:
  6.5 45.1 %all-gather.7.cloned.1.call-start = ((), (), s32[]{:S(2)}) async-start(), calls=%async_computation.1 | async-start | bytes 1966080 | tf_op jit(solution)/shard_map/all_gather | solution.py:26
  11.7 48.6 %copy-start.2 = (f32[128]{0:T(128)S(1)}, f32[128]{0:T(128)}, u32[]{:S(2)}) copy-start(f32[128]{0:T(128)} %param.15) | copy-start | bytes 1540
  11.7 48.6 %copy-start.3 = (f32[128]{0:T(128)S(1)}, f32[128]{0:T(128)}, u32[]{:S(2)}) copy-start(f32[128]{0:T(128)} %param.16) | copy-start | bytes 1540
  11.7 79.8 %all-gather.13.cloned.1.call-start = ((), (), s32[]{:S(2)}) async-start(), calls=%async_computation.4 | async-start | bytes 3538944 | tf_op jit(solution)/shard_map/all_gather | solution.py:42
  60.3 65.3 %all-gather.11.cloned.1.call-start = ((), (), s32[]{:S(2)}) async-start(), calls=%async_computation.3 | async-start | bytes 3538944 | tf_op jit(solution)/shard_map/all_gather | solution.py:41
  69.4 118.0 %all-gather.9.cloned.1.call-start = ((), (), s32[]{:S(2)}) async-start(), calls=%async_computation.2 | async-start | bytes 1966080 | tf_op jit(solution)/shard_map/all_gather | solution.py:70
  205.6 1.0 copy-start
  205.6 1.0 copy-start.1
Sparse Core Ops, SparseCore 0:
  11.8 39.7 all-gather.6
  60.4 31.0 all-gather.12
  93.4 32.1 all-gather.10
  150.4 37.0 all-gather.8
where the time goes:
time: 215 us; the launch traced here: 214 us
  waiting for transfers between devices  133 us (62%)
  matrix products  21 us (10%)
  local copies, waits for them, and re-layouts  19.7 us (9%)
  blocking collectives  13.9 us (6%)
  between operations  13.3 us (6%)
  other arithmetic  12.5 us (6%)
    all_gather x1, waiting for transfers between devices, local(): lax.all_gather(modulated, 'ulysses', axis=0, tiled=True)  39.8 us
    all_gather x1, waiting for transfers between devices, local(): lax.all_gather(attended, 'ulysses', axis=1, tiled=True)  37.2 us
    all_gather x1, waiting for transfers between devices, local(): key_part = lax.all_gather(keys, 'blk', axis=0, tiled=True)  34.1 us
    all_gather x1, waiting for transfers between devices, local(): value_part = lax.all_gather(values, 'blk', axis=0, tiled=True)  21.6 us
    all_to_all x1, blocking collectives, local(): lax.all_to_all(columns.astype(jnp.bfloat16), 'ulysses', split_axis=0, con...  13.9 us
    dynamic_slice x16, local copies, waits for them, and re-layouts, step(): lax.dynamic_slice_in_dim(value_part, position * query_rows, query_rows, 0)  10.7 us
    dot_general x1, matrix products, local(): jnp.einsum('rd,jde->jre', lax.all_gather(modulated, 'ulysses', axis=0, ti...  7.86 us
    dot_general x8, matrix products, step(): jnp.einsum('hqk,khd->hqd', powers.astype(jnp.bfloat16), value_block, pref...  5.52 us
  transfers between devices with their start and end apart: 4, of which 4 were waited for; matrix products, arithmetic and copies ran while one was open for 4% of the time, Pallas kernels for 0%

commit v1 on v0

--- a/solution.py
+++ b/solution.py
@@ -38,8 +38,9 @@
         jnp.zeros((heads_here, query_rows), jnp.float32),
         jnp.zeros((heads_here, query_rows, head_size), jnp.float32),
     )
-    key_part = lax.all_gather(keys, "blk", axis=0, tiled=True)
-    value_part = lax.all_gather(values, "blk", axis=0, tiled=True)
+    out_arr = jnp.concatenate([keys, values], 1)
+    field_out = lax.all_gather(out_arr, "blk", axis=0, tiled=True)
+    key_part, value_part = jnp.split(field_out, [keys.shape[1]], axis=1)
     count = key_part.shape[0] // query_rows
 
     def step(position, state):

time: 215 us -> 223 us (1.037)
  local copies, waits for them, and re-layouts: 19.7 us -> 33.5 us
  waiting for transfers between devices: 133 us -> 121 us
  other arithmetic: 12.5 us -> 17.5 us
    all_gather x2 -> x1, waiting for transfers between devices: 55.7 us -> 43.9 us  [local(): field_out = lax.all_gather(out_arr, 'blk', axis=0, tiled=True)]
    while x8 -> x56, local copies, waits for them, and re-layouts: 0.02 us -> 8.29 us
    split x0 -> x1, local copies, waits for them, and re-layouts: none -> 5.88 us  [local(): key_part, value_part = jnp.split(field_out, [keys.shape[1]], axis=1)]
    add x8, other arithmetic: 0.1 us -> 4.95 us  [step(): total = total * rescale + jnp.sum(powers, axis=-1)]
  transfers between devices with their start and end apart: 4 -> 3, of which waited for: 4 -> 3; matrix products, arithmetic and copies ran while one was open for 4% -> 0% of each run, Pallas kernels for 0% -> 0%
where the time goes in v1:
time: 223 us; the launch traced here: 221 us
  waiting for transfers between devices  121 us (54%)
  local copies, waits for them, and re-layouts  33.5 us (15%)
  matrix products  21 us (9%)
  other arithmetic  17.5 us (8%)
  blocking collectives  13.9 us (6%)
  between operations  13.3 us (6%)
    all_gather x1, waiting for transfers between devices, local(): field_out = lax.all_gather(out_arr, 'blk', axis=0, tiled=True)  43.9 us
    all_gather x1, waiting for transfers between devices, local(): lax.all_gather(modulated, 'ulysses', axis=0, tiled=True)  39.8 us
    all_gather x1, waiting for transfers between devices, local(): lax.all_gather(attended, 'ulysses', axis=1, tiled=True)  37.2 us
    all_to_all x1, blocking collectives, local(): lax.all_to_all(columns.astype(jnp.bfloat16), 'ulysses', split_axis=0, con...  13.9 us
    dynamic_slice x16, local copies, waits for them, and re-layouts, step(): lax.dynamic_slice_in_dim(value_part, position * query_rows, query_rows, 0)  10.7 us
    while x56, local copies, waits for them, and re-layouts  8.29 us
    dot_general x1, matrix products, local(): jnp.einsum('rd,jde->jre', lax.all_gather(modulated, 'ulysses', axis=0, ti...  7.86 us
    split x1, local copies, waits for them, and re-layouts, local(): key_part, value_part = jnp.split(field_out, [keys.shape[1]], axis=1)  5.88 us
  transfers between devices with their start and end apart: 3, of which 3 were waited for; matrix products, arithmetic and copies ran while one was open for 0% of the time, Pallas kernels for 0%

profile of v1, /device:TPU:0, one launch (start us, length us, event | category | flops | bytes accessed | tf_op | source)
XLA Modules:
  0.0 221.2 jit_solution(2813152202219448426)
XLA Ops:
  6.5 1.2 convert_reduce_fusion
  7.7 1.3 fusion.9
  9.0 0.7 broadcast_add_fusion
  9.7 2.0 fusion.12
  11.8 39.8 %all-gather.4.cloned.1.call-done = bf16[256,3072]{1,0:T(8,128)(2,1)} async-done(((bf16[64,3072]{1,0:T(8,128)(2,1)}), bf16[256,3072]{1,0:T(8,128)(2,1)}) %all-gather.4.cloned.1.call-update) | async-done | bytes 1572880 | tf_op jit(solution)/shard_map/all_gather | solution.py:26
  51.6 7.9 %convolution_bitcast_fusion = f32[3,256,768]{2,1,0:T(8,128)S(1)} fusion(bf16[3,3072,768]{2,1,0:T(8,128)(2,1)} %param.14, bf16[256,3072]{1,0:T(8,128)(2,1)} %all-gather.4.cloned.1.call-done), kind=kOutput, calls=%fused_computation.14 | convolution fusion | flops 3623878656 | bytes 18087936 | tf_op jit(solution)/shard_map/rd,jde->jre/dot_general | solution.py:24
  59.5 1.3 slice_multiply_fusion
  60.8 1.4 copy.28
  62.3 1.2 copy.29
  63.5 1.4 copy.30
  65.1 1.2 copy.31
  66.2 1.6 multiply_convert_fusion
  67.8 0.9 pad_maximum_fusion
  69.2 43.9 %all-gather.6.cloned.1.call-done = bf16[2048,1536]{1,0:T(8,128)(2,1)} async-done(((bf16[256,1536]{1,0:T(8,128)(2,1)}), bf16[2048,1536]{1,0:T(8,128)(2,1)}) %all-gather.6.cloned.1.call-update) | async-done | bytes 6291472 | tf_op jit(solution)/shard_map/all_gather | solution.py:42
  113.2 5.9 %fusion.16 = (bf16[2048,768]{1,0:T(8,128)(2,1)}, bf16[2048,768]{1,0:T(8,128)(2,1)}) fusion(bf16[2048,1536]{1,0:T(8,128)(2,1)} %all-gather.6.cloned.1.call-done), kind=kLoop, calls=%fused_computation.44 | loop fusion | bytes 12582912 | tf_op jit(solution)/shard_map/split | solution.py:43
  119.0 36.9 %while.18 = (s32[]{:T(128)}, f32[6,256]{1,0:T(8,128)S(1)}, f32[6,256]{1,0:T(8,128)}, f32[6,256,128]{2,1,0:T(8,128)S(1)}, bf16[2048,768]{1,0:T(8,128)(2,1)}, /*in...) while((s32[]{:T(128)}, f32[6,256]{1,0:T(8,128)S(1)}, ...), condition=%wide.region_7.0_spmd.clone, body=%wide.region_4.0_spmd.clone.sunk | while | flops 203890176 | bytes 10789119 | solution.py:67
  119.0 1.2 constant_dynamic-slice_fusion.3
  122.3 0.7 convolution_add_fusion.2
  123.1 1.2 constant_dynamic-slice_fusion.3
  125.5 0.7 fusion.34
  126.3 0.6 copy-done.3
  127.0 0.7 convolution_add_fusion.2
  127.8 1.2 constant_dynamic-slice_fusion.3
  130.2 0.7 fusion.34
  131.0 0.6 copy-done.3
  131.7 0.7 convolution_add_fusion.2
  132.5 1.2 constant_dynamic-slice_fusion.3
  134.9 0.7 fusion.34
  136.4 0.7 convolution_add_fusion.2
  137.2 1.2 constant_dynamic-slice_fusion.3
  139.6 0.7 fusion.34
  140.4 0.6 copy-done.3
  141.1 0.7 convolution_add_fusion.2
  141.9 1.2 constant_dynamic-slice_fusion.3
  144.3 0.7 fusion.34
  145.8 0.7 convolution_add_fusion.2
  146.6 1.2 constant_dynamic-slice_fusion.3
  149.0 0.7 fusion.34
  150.5 0.7 convolution_add_fusion.2
  151.3 1.2 constant_dynamic-slice_fusion.3
  153.8 0.7 fusion.34
  155.2 0.7 convolution_add_fusion.2
  156.6 0.8 divide_convert_fusion
  157.5 37.2 %all-gather.8.cloned.1.call-done = bf16[256,3072]{0,1:T(8,128)(2,1)} async-done(((bf16[256,768]{0,1:T(8,128)(2,1)}), bf16[256,3072]{0,1:T(8,128)(2,1)}) %all-gather.8.cloned.1.call-update) | async-done | bytes 1572880 | tf_op jit(solution)/shard_map/all_gather | solution.py:71
  194.7 4.2 %convolution_convert_fusion = bf16[256,768]{1,0:T(8,128)(2,1)S(1)} fusion(bf16[256,3072]{0,1:T(8,128)(2,1)} %all-gather.8.cloned.1.call-done, bf16[3072,768]{1,0:T(8,128)(2,1)} %param.17), kind=kOutput, calls=%fused_computation.16 | convolution fusion | flops 1208156160 | bytes 6684672 | tf_op jit(solution)/shard_map/dot_general | solution.py:70
  198.9 13.9 %all_to_all.13 = bf16[4,64,768]{2,1,0:T(8,128)(2,1)S(1)} all-to-all(bf16[4,64,768]{2,1,0:T(8,128)(2,1)S(1)} %bitcast.69), channel_id=1, replica_groups=mesh['blk'=8,'ulysses'=4] {'ulysses'}, dimensions={0} | all-to-all | bytes 786432 | tf_op jit(solution)/shard_map/all_to_all | solution.py:75
  213.0 0.9 copy-done
  213.8 0.8 fusion.13
  (127 shorter events, 16.1 us)
Async XLA Ops:
  6.5 5.2 %copy-start.6 = (f32[128]{0:T(128)S(1)}, f32[128]{0:T(128)}, u32[]{:S(2)}) copy-start(f32[128]{0:T(128)} %param.15) | copy-start | bytes 1540
  6.5 5.2 %copy-start.7 = (f32[128]{0:T(128)S(1)}, f32[128]{0:T(128)}, u32[]{:S(2)}) copy-start(f32[128]{0:T(128)} %param.16) | copy-start | bytes 1540
  6.5 45.1 %all-gather.4.cloned.1.call-start = ((), (), s32[]{:S(2)}) async-start(), calls=%async_computation.1 | async-start | bytes 1966080 | tf_op jit(solution)/shard_map/all_gather | solution.py:26
  11.7 101.4 %all-gather.6.cloned.1.call-start = ((), (), s32[]{:S(2)}) async-start(), calls=%async_computation.2 | async-start | bytes 7077888 | tf_op jit(solution)/shard_map/all_gather | solution.py:42
  68.8 125.9 %all-gather.8.cloned.1.call-start = ((), (), s32[]{:S(2)}) async-start(), calls=%async_computation.3 | async-start | bytes 1966080 | tf_op jit(solution)/shard_map/all_gather | solution.py:71
  119.0 1.8 copy-start.1
  120.8 0.7 copy-start.2
  121.5 0.6 copy-start.3
  123.0 1.8 copy-start.1
  124.8 0.7 copy-start.2
  126.2 0.6 copy-start.3
  127.7 1.8 copy-start.1
  129.5 0.7 copy-start.2
  130.9 0.6 copy-start.3
  132.4 1.8 copy-start.1
  134.2 0.7 copy-start.2
  135.6 0.6 copy-start.3
  137.1 1.8 copy-start.1
  138.9 0.7 copy-start.2
  140.4 0.6 copy-start.3
  141.8 1.8 copy-start.1
  143.6 0.7 copy-start.2
  145.1 0.6 copy-start.3
  146.5 1.8 copy-start.1
  148.3 0.7 copy-start.2
  149.8 0.6 copy-start.3
  151.2 1.8 copy-start.1
  153.0 0.7 copy-start.2
  154.5 0.6 copy-start.3
  155.9 0.7 copy-start.4
  212.8 1.0 copy-start
  212.8 1.0 copy-start.5
Sparse Core Ops, SparseCore 0:
  11.8 39.7 all-gather.3
  68.9 44.2 all-gather.5
  157.6 37.0 all-gather.7
